TPU v7x, 256 devices: a whole 4x4x8 slice. The times are simulated.
256 devices in a mesh: sub: 64 (over x, z, core), tile: 4 (over y).
Axes of the slice: x: 4, y: 4, z: 8, core: 2. Of those that a mesh axis runs over, the one named last changes fastest.
Arguments:
- coupling: bfloat16 [64, 28, 256, 256], P('sub'), may hold values from -0.125 to 0.125
- panel_inv: float32 [64, 8, 256, 256], P('sub')
- a_ib: bfloat16 [64, 2048, 3072], P('sub', None, 'tile'), may hold values from -0.5 to 0.5
- owner: int32 [64, 12, 12], P('sub', None, 'tile'), may hold values from 0 to 63, as said below
- slot: int32 [64, 12, 12], P('sub', None, 'tile'), may hold values from 0 to 15
- base: bfloat16 [64, 64, 256, 256], P('sub', 'tile'), may hold values from -2 to 2
Outputs:
- assembled: bfloat16 [64, 64, 256, 256], P('sub', 'tile')
Inputs may be any that keep to these rules, and one draw needn't show every extreme that they name: `owner`: tiles of one device are those of one subdomain s and tile columns t*12/4 to (t+1)*12/4 - 1. At most 1 tiles of one device name one sub index; for each t one sub index, drawn from the seed, is named by exactly 1 tiles of every device of that t.
All inputs are finite; a program needn't handle non-finite values.
Results may differ from a plain program's by a relative error of at most 0.0051.
Values may be sent and summed in bfloat16 or wider, within the bound.
A program may use at most 128 MiB of HBM per device.

v0:
```python
import jax
import jax.numpy as jnp
from jax import lax
from jax.sharding import Mesh
from jax.sharding import PartitionSpec as P

SUB = ("sub_0", "sub_1", "sub_2")


def split_up(array, dim, length):
    before, after = (array.shape[:dim], array.shape[dim + 1 :])
    return jnp.moveaxis(array.reshape(*before, length, -1, *after), dim, 0)


def joined_along(tiles, dim):
    dims = list(tiles.shape[1:])
    dims[dim] *= tiles.shape[0]
    return jnp.moveaxis(tiles, 0, dim).reshape(dims)


def exchange_in_order(tiles, axes, sequence):
    dims = [lax.axis_size(a) for a in axes]
    tiles = tiles.reshape(*dims, *tiles.shape[1:])
    for k in sequence:
        tiles = lax.all_to_all(tiles, axes[k], split_axis=k, concat_axis=k, tiled=True)
    return tiles.reshape(-1, *tiles.shape[len(axes) :])


def exchange_by_chip(array, groups, sequence, split_dim, concat_dim):
    length = lax.axis_size(groups[0]) * lax.axis_size(groups[1])
    tiles = split_up(array, split_dim, length)
    return joined_along(exchange_in_order(tiles, groups, sequence), concat_dim)


def solve(lower_blocks, inverse, right_cols):
    panel_width = inverse.shape[1]
    panels = []
    for row_panel in range(inverse.shape[0]):
        target = right_cols[row_panel * panel_width : (row_panel + 1) * panel_width].astype(
            jnp.float32
        )
        if row_panel > 0:
            block_start = row_panel * (row_panel - 1) // 2
            blocks = lower_blocks[block_start : block_start + row_panel]
            joined = jnp.transpose(blocks, (1, 0, 2)).reshape(panel_width, row_panel * panel_width)
            target = target - jnp.dot(
                joined, jnp.concatenate(panels, axis=0), preferred_element_type=jnp.float32
            )
        solved_panel = jnp.dot(
            inverse[row_panel],
            target,
            precision=lax.Precision.HIGHEST,
            preferred_element_type=jnp.float32,
        )
        panels.append(solved_panel.astype(jnp.bfloat16))
    return jnp.concatenate(panels, axis=0)


def inner_rows(left_part, right_part):
    return lax.dot_general(
        left_part, right_part, (((0,), (0,)), ((), ())), preferred_element_type=jnp.float32
    )


def shards(coupling, panel_inv, a_ib, owner, slot, base):
    lower_blocks = coupling[0]
    inverse = panel_inv[0]
    right_cols = a_ib[0]
    panel_width = inverse.shape[1]
    col_count = right_cols.shape[1]
    own_solved = solve(lower_blocks, inverse, right_cols)
    schur_cols = inner_rows(lax.all_gather(own_solved, "tile", axis=1, tiled=True), own_solved)
    tile_rows = schur_cols.shape[0] // panel_width
    col_tiles = col_count // panel_width
    tile_count = tile_rows * col_tiles
    contrib = (
        (-schur_cols).astype(jnp.bfloat16).reshape(tile_rows, panel_width, col_tiles, panel_width)
    )
    contrib = contrib.transpose(0, 2, 1, 3).reshape(tile_count, panel_width * panel_width)
    peer_count = lax.axis_size(SUB)
    capacity = (tile_count + peer_count - 1) // peer_count
    owners_flat = owner[0].reshape(tile_count)
    slot_flat = slot[0].reshape(tile_count)
    position = jnp.arange(tile_count, dtype=jnp.int32)
    matching = owners_flat[:, None] == owners_flat[None, :]
    earlier = position[None, :] < position[:, None]
    ranking = jnp.sum(jnp.where(matching & earlier, 1, 0), axis=1).astype(jnp.int32)
    target = owners_flat * capacity + ranking
    seat_index = jnp.arange(peer_count * capacity, dtype=jnp.int32)
    selector = seat_index[:, None] == target[None, :]
    outgoing = jnp.dot(
        selector.astype(jnp.bfloat16), contrib, preferred_element_type=jnp.float32
    ).astype(jnp.bfloat16)
    outgoing = outgoing.reshape(peer_count, capacity, panel_width * panel_width)
    labels = jnp.sum(jnp.where(selector, slot_flat[None, :] + 1, 0), axis=1) - 1
    labels = labels.reshape(peer_count, capacity)
    incoming, landed = (
        exchange_by_chip(outgoing, (("sub_0", "sub_1"), "sub_2"), (0, 1), 0, 0),
        exchange_by_chip(labels, (("sub_0", "sub_1"), "sub_2"), (0, 1), 0, 0),
    )
    slots_here = base.shape[1]
    landing = (
        jnp.arange(slots_here, dtype=jnp.int32)[:, None]
        == landed.reshape(peer_count * capacity)[None, :]
    ).astype(jnp.bfloat16)
    summed = jnp.dot(
        landing,
        incoming.reshape(peer_count * capacity, panel_width * panel_width),
        preferred_element_type=jnp.float32,
    )
    result = (
        base[0].reshape(slots_here, panel_width * panel_width).astype(jnp.float32) + summed
    ).astype(jnp.bfloat16)
    return result.reshape(1, slots_here, panel_width, panel_width)


def solution(mesh):
    torus = Mesh(
        mesh.devices.reshape(4, 8, 2, mesh.shape["tile"]), ("sub_0", "sub_1", "sub_2", "tile")
    )
    placed = (
        P(SUB, None, None, None),
        P(SUB, None, None, None),
        P(SUB, None, "tile"),
        P(SUB, None, "tile"),
        P(SUB, None, "tile"),
        P(SUB, "tile", None, None),
    )
    return jax.shard_map(
        shards, mesh=torus, in_specs=placed, out_specs=P(SUB, "tile", None, None), check_vma=False
    )
```

profile of v0, /device:TPU:32, one launch (start us, length us, event | category | flops | bytes accessed | tf_op | source)
XLA Modules:
  0.0 524.4 jit_solution(17396525251571783632)
XLA Ops:
  17.2 2.7 constant_dynamic-update-slice_fusion.17
  33.4 2.2 copy.95
  37.6 2.3 copy.97
  41.8 2.4 copy.99
  45.7 3.0 constant_dynamic-update-slice_fusion.16
  65.2 19.6 %all_to_all.20 = s32[32,2,1,1]{1,3,2,0:T(1,128)S(1)} all-to-all(s32[32,2,1,1]{1,3,2,0:T(1,128)S(1)} %bitcast.198), channel_id=1, replica_groups=mesh['sub_0'=4,'sub_1'=8,'sub_2'=2,'tile'=4] {'sub_0','sub_1'}, dimensions={0} | all-to-all | bytes 512 | tf_op jit(solution)/shard_map/all_to_all | solution.py:25
  85.4 3.2 all-to-all-start.1
  88.7 99.6 %all-gather.2.cloned.1.call-done = bf16[2048,3072]{1,0:T(8,128)(2,1)} async-done(((bf16[2048,768]{1,0:T(8,128)(2,1)}), bf16[2048,3072]{1,0:T(8,128)(2,1)}) %all-gather.2.cloned.1.call-update) | async-done | bytes 12582928 | tf_op jit(solution)/shard_map/all_gather | solution.py:72
  188.2 15.6 %negate_convert_fusion = bf16[3072,768]{1,0:T(8,128)(2,1)} fusion(bf16[2048,3072]{1,0:T(8,128)(2,1)} %all-gather.2.cloned.1.call-done, bf16[2048,768]{1,0:T(8,128)(2,1)} %copy-done), kind=kOutput, calls=%fused_computation.3 | convolution fusion | flops 9668395008 | bytes 20447232 | tf_op jit(solution)/shard_map/dot_general | solution.py:60
  203.8 6.7 %copy.82 = bf16[3072,768]{0,1:T(8,128)(2,1)} copy(bf16[3072,768]{1,0:T(8,128)(2,1)} %negate_convert_fusion) | data formatting | bytes 9437184 | tf_op jit(solution)/shard_map/convert_element_type | solution.py:77
  210.5 9.2 %reshape.112 = bf16[12,256,3,256]{1,0,3,2:T(8,128)(2,1)} reshape(bf16[3072,768]{0,1:T(8,128)(2,1)} %copy.82) | data formatting | bytes 9437184 | tf_op jit(solution)/shard_map/reshape | solution.py:77
  219.6 9.1 %copy.83 = bf16[12,3,256,256]{3,2,1,0:T(8,128)(2,1)} copy(bf16[12,3,256,256]{2,0,3,1:T(8,128)(2,1)} %bitcast.185) | data formatting | bytes 9437184 | tf_op jit(solution)/shard_map/transpose | solution.py:79
  228.7 2.9 pad.9
  231.6 3.1 copy.101
  234.7 5.7 %convolution_convert_fusion = bf16[64,65536]{1,0:T(8,128)(2,1)} fusion(bf16[36,65536]{1,0:T(8,128)(2,1)S(1)} %bitcast.187, s32[36]{0:T(128)S(1)} %add.33), kind=kOutput, calls=%fused_computation | convolution fusion | flops 306186496 | bytes 13107344 | tf_op jit(solution)/shard_map/dot_general | solution.py:91
  240.4 10.5 %reshape_reshape_reshape.7 = bf16[32,2,1,1,65536]{4,1,0,3,2:T(2,128)(2,1)} reshape(bf16[64,65536]{1,0:T(8,128)(2,1)} %convolution_convert_fusion) | data formatting | bytes 16777216 | tf_op jit(solution)/shard_map/reshape;reshape;reshape | solution.py:23
  251.0 10.7 %all-to-all-start.2 = ((bf16[32,2,1,1,65536]{4,1,3,2,0:T(2,128)(2,1)}), bf16[32,2,1,1,65536]{4,1,3,2,0:T(2,128)(2,1)}, u32[]{:S(2)}, u32[]{:S(2)}) async-start(bf16[32,2,1,1,65536]{4,1,3,2,0:T(2,128)(2,1)} %bitcast.184), calls=%async_computation.2 | async-start | bytes 16777216 | tf_op jit(solution)/shard_map/all_to_all | solution.py:25
  261.7 3.2 copy.100
  265.0 195.4 %all-to-all-done.2 = bf16[32,2,1,1,65536]{4,1,3,2,0:T(2,128)(2,1)} async-done(((bf16[32,2,1,1,65536]{4,1,3,2,0:T(2,128)(2,1)}), bf16[32,2,1,1,65536]{4,1,3,2,0:T(2,128)(2,1)}, u32[]{:S(2)}, u32[]{:S(2)}) %all-to-all-start.2) | async-done | bytes 8388640 | tf_op jit(solution)/shard_map/all_to_all | solution.py:25
  460.5 11.2 %copy.85 = bf16[32,2,1,1,65536]{4,0,3,2,1:T(8,128)(2,1)} copy(bf16[32,2,1,1,65536]{4,1,3,2,0:T(2,128)(2,1)} %all-to-all-done.2) | data formatting | bytes 16777216 | tf_op jit(solution)/shard_map/all_to_all | solution.py:25
  471.7 12.1 %all_to_all.21 = bf16[32,2,1,1,65536]{4,0,3,2,1:T(8,128)(2,1)S(1)} all-to-all(bf16[32,2,1,1,65536]{4,0,3,2,1:T(8,128)(2,1)} %copy.85), channel_id=1, replica_groups=mesh['sub_0'=4,'sub_1'=8,'sub_2'=2,'tile'=4] {'sub_2'}, dimensions={1} | all-to-all | bytes 16777216 | tf_op jit(solution)/shard_map/all_to_all | solution.py:25
  483.8 15.5 %copy.86 = bf16[32,2,1,1,65536]{4,1,0,3,2:T(2,128)(2,1)} copy(bf16[32,2,1,1,65536]{4,0,3,2,1:T(8,128)(2,1)S(1)} %all_to_all.21) | data formatting | bytes 16777216 | tf_op jit(solution)/shard_map/all_to_all | solution.py:25
  499.3 10.3 %reshape_reshape_reshape.8 = bf16[64,65536]{1,0:T(8,128)(2,1)} reshape(bf16[32,2,1,1,65536]{4,1,0,3,2:T(2,128)(2,1)} %copy.86) | data formatting | bytes 16777216 | tf_op jit(solution)/shard_map/reshape;reshape;reshape | solution.py:108
  509.6 5.8 %fusion = bf16[16,65536]{1,0:T(8,128)(2,1)S(1)} fusion(f32[16,65536]{1,0:T(8,128)} %bitcast.189, bf16[64,65536]{1,0:T(8,128)(2,1)} %reshape_reshape_reshape.8, s32[64]{0:T(128)S(1)} %eq.48), kind=kOutput, calls=%fused_computation.2 | convolution fusion | flops 136315904 | bytes 14680320 | tf_op jit(solution)/shard_map/dot_general | solution.py:106
  (96 shorter events, 48.4 us)
Async XLA Ops:
  6.5 181.7 %all-gather.2.cloned.1.call-start = ((), (), s32[]{:S(2)}) async-start(), calls=%async_computation.4 | async-start | bytes 15728640 | tf_op jit(solution)/shard_map/all_gather | solution.py:72
  6.5 8.1 %copy-start.1 = (bf16[1,28,256,256]{3,2,1,0:T(8,128)(2,1)S(1)}, bf16[1,28,256,256]{3,2,1,0:T(8,128)(2,1)}, u32[]{:S(2)}) copy-start(bf16[1,28,256,256]{3,2,1,0:T(8,128)(2,1)} %param.6) | copy-start | bytes 11010052
  8.5 7.2 %copy-start.2 = (bf16[1,2048,768]{2,1,0:T(8,128)(2,1)S(1)}, bf16[1,2048,768]{2,1,0:T(8,128)(2,1)}, u32[]{:S(2)}) copy-start(bf16[1,2048,768]{2,1,0:T(8,128)(2,1)} %param.8) | copy-start | bytes 9437188
  17.2 6.5 %slice-start = ((bf16[1,28,256,256]{3,2,1,0:T(8,128)(2,1)}), bf16[1,2,256,256]{3,2,1,0:T(8,128)(2,1)S(1)}, s32[]{:S(2)}) async-start(bf16[1,28,256,256]{3,2,1,0:T(8,128)(2,1)} %param.6), calls=%async_computation.5 | async-start | bytes 524288 | tf_op jit(solution)/shard_map/slice | solution.py:44
  24.6 7.9 %copy-start.6 = (bf16[1,256,768]{2,1,0:T(8,128)(2,1)S(1)}, bf16[1,256,768]{2,1,0:T(8,128)(2,1)}, u32[]{:S(2)}) copy-start(bf16[1,256,768]{2,1,0:T(8,128)(2,1)} %get-tuple-element.7) | copy-start | bytes 1179652
  35.6 8.6 %copy-start.5 = (bf16[256,768]{1,0:T(8,128)(2,1)S(1)}, bf16[256,768]{1,0:T(8,128)(2,1)}, u32[]{:S(2)}) copy-start(bf16[256,768]{1,0:T(8,128)(2,1)} %get-tuple-element.37) | copy-start | bytes 1179652
  44.2 4.4 copy-start.17
  44.2 4.4 copy-start.18
  45.7 3.4 copy-start.3
  48.7 2.3 copy-start.15
  48.7 2.3 copy-start.16
  51.0 2.3 copy-start.20
  51.5 3.3 copy-start.10
  51.5 3.3 copy-start.14
  54.9 1.8 copy-start.21
  54.9 2.6 copy-start.9
  54.9 2.6 copy-start.13
  59.2 1.7 copy-start.7
  59.2 1.7 copy-start.11
  61.8 2.5 copy-start.22
  61.8 2.9 copy-start.23
  85.4 165.5 %all-to-all-start.1 = ((s32[32,2,1,1]{0,3,2,1:T(1,128)}), s32[32,2,1,1]{0,3,2,1:T(1,128)S(1)}, u32[]{:S(2)}, u32[]{:S(2)}) async-start(s32[32,2,1,1]{0,3,2,1:T(1,128)} %copy.67), calls=%async_computation.1 | async-start | bytes 2048 | tf_op jit(solution)/shard_map/all_to_all | solution.py:25
  251.0 10.7 %copy-start.4 = (bf16[1,16,256,256]{3,2,1,0:T(8,128)(2,1)S(1)}, bf16[1,16,256,256]{3,2,1,0:T(8,128)(2,1)}, u32[]{:S(2)}) copy-start(bf16[1,16,256,256]{3,2,1,0:T(8,128)(2,1)} %param.11) | copy-start | bytes 6291460
  251.0 209.5 %all-to-all-start.2 = ((bf16[32,2,1,1,65536]{4,1,3,2,0:T(2,128)(2,1)}), bf16[32,2,1,1,65536]{4,1,3,2,0:T(2,128)(2,1)}, u32[]{:S(2)}, u32[]{:S(2)}) async-start(bf16[32,2,1,1,65536]{4,1,3,2,0:T(2,128)(2,1)} %bitcast.184), calls=%async_computation.2 | async-start | bytes 16777216 | tf_op jit(solution)/shard_map/all_to_all | solution.py:25
  (4 other events, 6.4 us)
Sparse Core Ops, SparseCore 0:
  64.5 123.6 all-gather.1
where the time goes:
time: 534 us; the launch traced here: 524 us
  waiting for transfers between devices  295 us (55%)
  local copies, waits for them, and re-layouts  124 us (23%)
  matrix products  45 us (8%)
  blocking collectives  31.7 us (6%)
  between operations  14.2 us (3%)
  starting transfers between devices  13.9 us (3%)
    all_to_all x2, waiting for transfers between devices, exchange_in_order(): lax.all_to_all(tiles, axes[k], split_axis=k, concat_axis=k, tiled=True)  195 us
    all_gather x1, waiting for transfers between devices, shards(): lax.all_gather(own_solved, 'tile', axis=1, tiled=True)  99.6 us
    unnamed x66, local copies, waits for them, and re-layouts  40 us
    all_to_all x2, blocking collectives, exchange_in_order(): lax.all_to_all(tiles, axes[k], split_axis=k, concat_axis=k, tiled=True)  31.7 us
    all_to_all x4, local copies, waits for them, and re-layouts, exchange_in_order(): lax.all_to_all(tiles, axes[k], split_axis=k, concat_axis=k, tiled=True)  27.5 us
    dot_general x1, matrix products, inner_rows(): lax.dot_general(left_part, right_part, (((0,), (0,)), ((), ())), preferre...  15.6 us
    all_to_all x2, starting transfers between devices, exchange_in_order(): lax.all_to_all(tiles, axes[k], split_axis=k, concat_axis=k, tiled=True)  13.9 us
    dot_general x8, matrix products, solve(): jnp.dot(inverse[row_panel], target, precision=lax.Precision.HIGHEST, pref...  12.6 us
  transfers between devices with their start and end apart: 3, of which 2 were waited for; matrix products, arithmetic and copies ran while one was open for 13% of the time, Pallas kernels for 0%

commit v1 on v0

v1 whole, which is shorter than its diff:
```python
import functools

import jax
import jax.numpy as jnp
from jax import lax
from jax.experimental import pallas as pl
from jax.experimental.pallas import tpu as pltpu
from jax.sharding import PartitionSpec as P

MESH = pl.DeviceIdType.MESH
NX, NZ, NC, NY = 4, 8, 2, 4
PW = 256
NQ = 16
R = PW // NQ
VMEM_LIMIT = 67043328
NT = (((1,), (1,)), ((), ()))


def dot_nt(left, right):
    return lax.dot_general(left, right, NT, preferred_element_type=jnp.float32)


def split_hi_lo(value):
    high = value.astype(jnp.bfloat16)
    low = (value - high.astype(jnp.float32)).astype(jnp.bfloat16)
    return high, low


def solve_kernel(owner_s, slot_s, c_ref, inv_ref, a_ref, y_ref, idx_s, pages_ref, lab_s):
    t = lax.axis_index("tile")
    for j in range(64):
        idx_s[j] = 36
        lab_s[j] = -1
    for a in range(12):
        d = lax.rem(a // 3 - t + NY, NY)
        rel = jnp.where(d == 0, 0, jnp.where(d == 3, 1, jnp.where(d == 1, 2, 3)))
        for b in range(3):
            o = owner_s[a, b]
            seat = ((o // 16) * 2 + lax.rem(o, 2)) * 8 + lax.rem(o // 2, 8)
            idx_s[seat] = (rel * 3 + a % 3) * 3 + b
            lab_s[seat] = slot_s[a, b]
    for j in range(64):
        pages_ref[j // 8, j % 8] = jnp.full((8, 128), lab_s[j], jnp.int32)
    for k in range(8):
        target = a_ref[k * PW : (k + 1) * PW, :].astype(jnp.float32).T
        if k:
            start = k * (k - 1) // 2
            joined = jnp.concatenate([c_ref[start + m] for m in range(k)], axis=1)
            target = target - dot_nt(y_ref[:, : k * PW], joined)
        t_hi, t_lo = split_hi_lo(target)
        i_hi, i_lo = split_hi_lo(inv_ref[k])
        solved = dot_nt(
            jnp.concatenate([t_hi, t_hi, t_lo], axis=1), jnp.concatenate([i_hi, i_lo, i_hi], axis=1)
        )
        y_ref[:, k * PW : (k + 1) * PW] = solved.astype(jnp.bfloat16)


def combine(dense, tiles, write):
    for half in range(2):
        cols = slice(half * 128, half * 128 + 128)
        acc = [None] * 16
        for view in dense:
            for j in range(16):
                x = view(j, cols).astype(jnp.float32)
                acc[j] = x if acc[j] is None else acc[j] + x
        for view, page in tiles:
            x = view(cols).astype(jnp.float32)
            lab = page()
            lab = jnp.concatenate([lab] * (R // 8), axis=0)
            for j in range(16):
                term = jnp.where(lab == j, x, 0.0)
                acc[j] = term if acc[j] is None else acc[j] + term
        for j in range(16):
            write(j, cols, acc[j])


def exchange_kernel(
    idx_s, pages, own, base, out,
    G, S, RA, T, B1, B2, B3, B4, C3, C4, tiles, RL, L1, L2,
    sy, ry, sa, sf, ra, rt, sz, rz, sl, rl, rlz,
):
    s = lax.axis_index("sub")
    t = lax.axis_index("tile")
    x, z, c = s // 16, lax.rem(s // 2, NZ), lax.rem(s, 2)
    g_own = x * 2 + c

    def at(dx, dz, core, dt):
        xx = lax.rem(x + dx + NX, NX)
        zz = lax.rem(z + dz + NZ, NZ)
        return ((xx * NZ + zz) * NC + core, lax.rem(t + dt + NY, NY))

    def group(dx, core):
        return lax.rem(x + dx + NX, NX) * 2 + core

    def zat(dz):
        return lax.rem(z + dz + NZ, NZ)

    def rc(src, dst, ss, rs, dev):
        return pltpu.make_async_remote_copy(
            src_ref=src, dst_ref=dst, send_sem=ss, recv_sem=rs, device_id=dev, device_id_type=MESH
        )

    direct = [(1, 0), (1, 1), (-1, 0), (-1, 1), (0, 1 - c)]
    two = [(2, 0), (2, 1)]

    def y_direct(q, i):
        return rc(own.at[:, q], G.at[q, i], sy.at[q, i], ry.at[q, i], at(0, 0, c, (1, -1)[i]))

    def y_forward(q, i):
        lanes = pl.ds(i * 1024, 1024)
        return rc(
            G.at[q, i, :, :, lanes], G.at[q, 2, :, :, lanes],
            sy.at[q, 2 + i], ry.at[q, 2 + i], at(0, 0, c, (1, -1)[i]),
        )

    def a_direct(q, i):
        dx, core = direct[i]
        return rc(
            S.at[q, group(dx, core)], RA.at[q, :, g_own], sa.at[q, i], ra.at[q, g_own], at(dx, 0, core, 0)
        )

    def a_transit(q, i):
        return rc(
            S.at[q, group(2, i)], T.at[q, i], sa.at[q, 5 + i], rt.at[q, i], at((1, -1)[i], 0, c, 0)
        )

    def a_forward(q, i):
        src_g = group((-1, 1)[i], c)
        return rc(
            T.at[q, i], RA.at[q, :, src_g], sf.at[q, i], ra.at[q, src_g], at((1, -1)[i], 0, i, 0)
        )

    def a_arrival(q, g):
        return rc(S.at[q, g], RA.at[q, :, g], sa.at[q, 0], ra.at[q, g], at(0, 0, 1 - c, 0))

    def z_copy(q, d, h):
        sign = 1 - 2 * d
        dev = at(0, sign, c, 0)
        if h == 0:
            src, dst = RA.at[q, zat(4), pl.ds(4 * d, 4)], B1.at[d, q]
        elif h == 1:
            src, dst = B1.at[d, q], B2.at[d, q, pl.ds(0, 4)]
        elif h == 2:
            src, dst = RA.at[q, zat(3 * sign)], B2.at[d, q, pl.ds(4, 8)]
        elif h == 3:
            src, dst = C3.at[d, q], B3.at[d, q]
        else:
            src, dst = C4.at[d, q], B4.at[d, q]
        return rc(src, dst, sz.at[q, d * 5 + h], rz.at[q, d * 5 + h], dev)

    def label_group(i):
        dx, core = (direct + two)[i]
        return rc(pages.at[group(dx, core)], RL.at[:, g_own], sl.at[i], rl.at[g_own], at(dx, 0, core, 0))

    def label_arrival(g):
        return rc(pages.at[g], RL.at[:, g], sl.at[0], rl.at[g], at(0, 0, 1 - c, 0))

    def label_z(d, i):
        sign = 1 - 2 * d
        if i == 0:
            src, dst = RL.at[zat(3 * sign)], L1.at[d]
        else:
            src, dst = RL.at[zat(4), pl.ds(4 * d, 4)], L2.at[d]
        return rc(src, dst, sl.at[7 + 2 * d + i], rlz.at[2 * d + i], at(0, sign * (1 + i), c, 0))

    barrier = pltpu.get_barrier_semaphore()
    peers = [at(dx, 0, core, 0) for dx, core in direct + two]
    peers += [at(0, dz, c, 0) for dz in (1, -1, 2, -2)] + [at(0, 0, c, dt) for dt in (1, -1)]
    for dev in peers:
        pl.semaphore_signal(barrier, inc=1, device_id=dev, device_id_type=MESH)
    pl.semaphore_wait(barrier, len(peers))

    for i in range(2):
        y_direct(0, i).start()
    for i in range(7):
        label_group(i).start()
    tiles[36] = jnp.zeros((R, PW), jnp.bfloat16)
    for zz in range(NZ):
        RL[zz, g_own] = pages[g_own, zz]
    for i in range(1, 8):
        label_arrival(lax.rem(g_own + i, 8)).wait_recv()
    for d in range(2):
        for i in range(2):
            label_z(d, i).start()
    for i in range(2):
        y_direct(0, i).wait_recv()
        y_forward(0, i).start()
    for q in (1, 2):
        for i in range(2):
            y_direct(q, i).start()
    for d in range(2):
        for i in range(2):
            label_z(d, i).wait_recv()

    def tile_view(ref, *index):
        return lambda cols: ref[(*index, slice(None), cols)]

    def page_view(ref, *index):
        return lambda: ref[index]

    def tick(step, carry):
        def stage(lag, run):
            q = step - lag

            @pl.when(jnp.logical_and(q >= 0, q < NQ))
            def _():
                run(q)

        def finish(q):
            for d in range(2):
                z_copy(q, d, 4).wait_recv()
            rows = pl.ds(pl.multiple_of(q * R, R), R)

            def write(j, cols, value):
                out[j, rows, cols] = value.astype(jnp.bfloat16)

            combine(
                [lambda j, cols: base[j, rows, cols]]
                + [lambda j, cols, d=d: B4[d, q, j, :, cols] for d in range(2)],
                [(tile_view(RA, q, z, g), page_view(RL, z, g)) for g in range(8)],
                write,
            )

        def hop4(q):
            for d in range(2):
                sign = 1 - 2 * d
                z_copy(q, d, 3).wait_recv()

                def write(j, cols, value, d=d):
                    C4[d, q, j, :, cols] = value.astype(jnp.bfloat16)

                combine(
                    [lambda j, cols, d=d: B3[d, q, j, :, cols]],
                    [(tile_view(RA, q, zat(sign), g), page_view(RL, zat(sign), g)) for g in range(8)],
                    write,
                )
                z_copy(q, d, 4).start()

        def hop3(q):
            for d in range(2):
                sign = 1 - 2 * d
                z_copy(q, d, 1).wait_recv()
                z_copy(q, d, 2).wait_recv()

                def write(j, cols, value, d=d):
                    C3[d, q, j, :, cols] = value.astype(jnp.bfloat16)

                combine(
                    [],
                    [(tile_view(B2, d, q, i), page_view(L2, d, i)) for i in range(4)]
                    + [(tile_view(B2, d, q, 4 + i), page_view(L1, d, i)) for i in range(8)]
                    + [(tile_view(RA, q, zat(2 * sign), g), page_view(RL, zat(2 * sign), g)) for g in range(8)],
                    write,
                )
                z_copy(q, d, 3).start()

        def hop2(q):
            for d in range(2):
                z_copy(q, d, 0).wait_recv()
                z_copy(q, d, 1).start()
                z_copy(q, d, 2).start()

        def hop1(q):
            for i in range(1, 8):
                a_arrival(q, lax.rem(g_own + i, 8)).wait_recv()
            for d in range(2):
                z_copy(q, d, 0).start()

        def relay(q):
            for i in range(2):
                a_transit(q, i).wait_recv()
                a_forward(q, i).start()

        def form(q):
            for i in range(2):
                y_forward(q, i).wait_recv()
            left = jnp.concatenate(
                [own[:, q].reshape(3 * R, 2048), G[q].reshape(9 * R, 2048)], axis=0
            )
            for b in range(3):
                gram = dot_nt(left, own[b].reshape(PW, 2048))
                for p in range(12):
                    tiles[p * 3 + b] = (-gram[p * R : (p + 1) * R]).astype(jnp.bfloat16)
            for j in range(64):
                S[q, j // 8, j % 8] = tiles[idx_s[j]]
            for i in range(2):
                a_transit(q, i).start()
            for i in range(5):
                a_direct(q, i).start()
            for zz in range(NZ):
                RA[q, zz, g_own] = S[q, g_own, zz]

        def gather(q):
            for i in range(2):
                y_direct(q, i).wait_recv()
                y_forward(q, i).start()

        def lead(q):
            for i in range(2):
                y_direct(q, i).start()

        stage(6, finish)
        stage(5, hop4)
        stage(4, hop3)
        stage(3, hop2)
        stage(2, hop1)
        stage(1, relay)
        stage(0, form)

        @pl.when(step + 1 < NQ)
        def _():
            gather(step + 1)

        @pl.when(step + 3 < NQ)
        def _():
            lead(step + 3)

        return carry

    lax.fori_loop(0, NQ + 6, tick, 0)

    def drain(q, carry):
        for i in range(2):
            y_direct(q, i).wait_send()
            y_forward(q, i).wait_send()
            a_transit(q, i).wait_send()
            a_forward(q, i).wait_send()
        for i in range(5):
            a_direct(q, i).wait_send()
        for d in range(2):
            for h in range(5):
                z_copy(q, d, h).wait_send()
        return carry

    lax.fori_loop(0, NQ, drain, 0)
    for i in range(7):
        label_group(i).wait_send()
    for d in range(2):
        for i in range(2):
            label_z(d, i).wait_send()


def shards(coupling, panel_inv, a_ib, owner, slot, base):
    vmem = pl.BlockSpec(memory_space=pltpu.VMEM)
    smem = pl.BlockSpec(memory_space=pltpu.SMEM)
    bf16, i32 = jnp.bfloat16, jnp.int32
    solved, idx, pages = pl.pallas_call(
        solve_kernel,
        out_shape=(
            jax.ShapeDtypeStruct((768, 2048), bf16),
            jax.ShapeDtypeStruct((64,), i32),
            jax.ShapeDtypeStruct((8, 8, 8, 128), i32),
        ),
        in_specs=[smem, smem, vmem, vmem, vmem],
        out_specs=(vmem, smem, vmem),
        scratch_shapes=[pltpu.SMEM((64,), i32)],
        compiler_params=pltpu.CompilerParams(vmem_limit_bytes=VMEM_LIMIT),
        name="solve",
    )(owner[0], slot[0], coupling[0], panel_inv[0], a_ib[0])
    dma = pltpu.SemaphoreType.DMA
    result = pl.pallas_call(
        exchange_kernel,
        out_shape=jax.ShapeDtypeStruct((16, PW, PW), bf16),
        in_specs=[smem, vmem, vmem, vmem],
        out_specs=vmem,
        scratch_shapes=[
            pltpu.VMEM((NQ, 3, 3, R, 2048), bf16),
            pltpu.VMEM((NQ, 8, 8, R, PW), bf16),
            pltpu.VMEM((NQ, 8, 8, R, PW), bf16),
            pltpu.VMEM((NQ, 2, 8, R, PW), bf16),
            pltpu.VMEM((2, NQ, 4, R, PW), bf16),
            pltpu.VMEM((2, NQ, 12, R, PW), bf16),
            pltpu.VMEM((2, NQ, 16, R, PW), bf16),
            pltpu.VMEM((2, NQ, 16, R, PW), bf16),
            pltpu.VMEM((2, NQ, 16, R, PW), bf16),
            pltpu.VMEM((2, NQ, 16, R, PW), bf16),
            pltpu.VMEM((37, R, PW), bf16),
            pltpu.VMEM((8, 8, 8, 128), i32),
            pltpu.VMEM((2, 8, 8, 128), i32),
            pltpu.VMEM((2, 4, 8, 128), i32),
            dma((NQ, 4)), dma((NQ, 4)),
            dma((NQ, 7)), dma((NQ, 2)), dma((NQ, 8)), dma((NQ, 2)),
            dma((NQ, 10)), dma((NQ, 10)),
            dma((11,)), dma((8,)), dma((4,)),
        ],
        compiler_params=pltpu.CompilerParams(
            collective_id=0, has_side_effects=True, vmem_limit_bytes=VMEM_LIMIT
        ),
        name="exchange",
    )(idx, pages, solved.reshape(3, NQ, R, 2048), base[0])
    return result[None]


def solution(mesh):
    placed = (
        P("sub", None, None, None),
        P("sub", None, None, None),
        P("sub", None, "tile"),
        P("sub", None, "tile"),
        P("sub", None, "tile"),
        P("sub", "tile", None, None),
    )
    return jax.shard_map(
        shards, mesh=mesh, in_specs=placed, out_specs=P("sub", "tile", None, None), check_vma=False
    )
```

time: 534 us -> 212 us (0.40); the launches traced: 524 us -> 212 us
  waiting for transfers between devices: 295 us -> 0 us
  Pallas kernels: 0 us -> 206 us
  local copies, waits for them, and re-layouts: 124 us -> 5.81 us
  matrix products: 45 us -> 0 us
  blocking collectives: 31.7 us -> 0 us
  between operations: 14.2 us -> 0.02 us
  starting transfers between devices: 13.9 us -> 0 us
    pallas_call x0 -> x2, Pallas kernels: none -> 206 us  [the longest x1 193 us: shards(): pl.pallas_call(exchange_kernel, out_shape=jax.ShapeDtypeStruct((16, PW, P...]
    all_to_all x2 -> x0, waiting for transfers between devices: 195 us -> none  [exchange_in_order(): lax.all_to_all(tiles, axes[k], split_axis=k, concat_axis=k, tiled=True)]
    all_gather x1 -> x0, waiting for transfers between devices: 99.6 us -> none  [shards(): lax.all_gather(own_solved, 'tile', axis=1, tiled=True)]
    dot_general x18 -> x0, matrix products: 45 us -> none  [the longest x1 15.6 us: inner_rows(): lax.dot_general(left_part, right_part, (((0,), (0,)), ((), ())), preferre...]
    unnamed x66 -> x1, local copies, waits for them, and re-layouts: 40 us -> 3.1 us
    all_to_all x2 -> x0, blocking collectives: 31.7 us -> none  [exchange_in_order(): lax.all_to_all(tiles, axes[k], split_axis=k, concat_axis=k, tiled=True)]
    all_to_all x4 -> x0, local copies, waits for them, and re-layouts: 27.5 us -> none  [exchange_in_order(): lax.all_to_all(tiles, axes[k], split_axis=k, concat_axis=k, tiled=True)]
    another operation x3 -> x0, local copies, waits for them, and re-layouts: 20.9 us -> none  [the longest x1 10.5 us: exchange_in_order(): tiles = tiles.reshape(*dims, *tiles.shape[1:])]
  transfers between devices with their start and end apart: 3 -> 0, of which waited for: 2 -> 0; matrix products, arithmetic and copies ran while one was open for 13% -> 0% of each run, Pallas kernels for 0% -> 0%
where the time goes in v1:
time: 212 us
  Pallas kernels  206 us (97%)
  local copies, waits for them, and re-layouts  5.81 us (3%)
    pallas_call x1, Pallas kernels, shards(): pl.pallas_call(exchange_kernel, out_shape=jax.ShapeDtypeStruct((16, PW, P...  193 us
    pallas_call x1, Pallas kernels, shards(): pl.pallas_call(solve_kernel, out_shape=(jax.ShapeDtypeStruct((768, 2048),...  13.5 us

profile of v1, /device:TPU:32, one launch (start us, length us, event | category | flops | bytes accessed | tf_op | source)
XLA Modules:
  0.0 212.0 jit_solution(5240081480089522692)
XLA Ops:
  0.0 1.4 copy.9
  1.4 1.4 copy.10
  2.7 13.5 %solve.1 = (bf16[768,2048]{1,0:T(8,128)(2,1)}, s32[64]{0:T(128)}, s32[8,8,8,128]{3,2,1,0:T(8,128)}) custom-call(s32[12,3]{1,0:T(8,128)} %bitcast.14, s32[12,3]{1,0:T(8,128)} %bitcast.15, bf16[28,256,256]{2,1,0:T(8,128)(2,1)} %bitcast.9, f32[8,256,256]{2,1,0:T(8,128)} %bitcast.12, bf16[2048,768]{1,0:T(8,128)(2,1)} %bitcast.10), custom_call_target="tpu_custom_call" | custom-call | tf_op jit(solution)/shard_map/solve/pallas_call | solution.py:347
  16.3 192.7 %exchange.1 = bf16[16,256,256]{2,1,0:T(8,128)(2,1)} custom-call(s32[64]{0:T(128)} %get-tuple-element.8.idx_s, s32[8,8,8,128]{3,2,1,0:T(8,128)} %get-tuple-element.9.pages, bf16[3,16,16,2048]{3,2,1,0:T(8,128)(2,1)} %bitcast.11, bf16[16,256,256]{2,1,0:T(8,128)(2,1)} %bitcast.13), custom_call_target="tpu_custom_call" | custom-call | tf_op jit(solution)/shard_map/exchange/pallas_call | solution.py:361
  208.9 3.1 %copy.12 = bf16[1,16,256,256]{3,2,1,0:T(8,128)(2,1)} copy(bf16[1,16,256,256]{3,2,1,0:T(8,128)(2,1)} %bitcast.8) | data formatting | bytes 4194304

commit v2 on v1

--- a/solution.py
+++ b/solution.py
@@ -12,6 +12,8 @@
 PW = 256
 NQ = 16
 R = PW // NQ
+FIRST = 4
+RING = 4
 VMEM_LIMIT = 67043328
 NT = (((1,), (1,)), ((), ()))
 
@@ -24,35 +26,6 @@
     high = value.astype(jnp.bfloat16)
     low = (value - high.astype(jnp.float32)).astype(jnp.bfloat16)
     return high, low
-
-
-def solve_kernel(owner_s, slot_s, c_ref, inv_ref, a_ref, y_ref, idx_s, pages_ref, lab_s):
-    t = lax.axis_index("tile")
-    for j in range(64):
-        idx_s[j] = 36
-        lab_s[j] = -1
-    for a in range(12):
-        d = lax.rem(a // 3 - t + NY, NY)
-        rel = jnp.where(d == 0, 0, jnp.where(d == 3, 1, jnp.where(d == 1, 2, 3)))
-        for b in range(3):
-            o = owner_s[a, b]
-            seat = ((o // 16) * 2 + lax.rem(o, 2)) * 8 + lax.rem(o // 2, 8)
-            idx_s[seat] = (rel * 3 + a % 3) * 3 + b
-            lab_s[seat] = slot_s[a, b]
-    for j in range(64):
-        pages_ref[j // 8, j % 8] = jnp.full((8, 128), lab_s[j], jnp.int32)
-    for k in range(8):
-        target = a_ref[k * PW : (k + 1) * PW, :].astype(jnp.float32).T
-        if k:
-            start = k * (k - 1) // 2
-            joined = jnp.concatenate([c_ref[start + m] for m in range(k)], axis=1)
-            target = target - dot_nt(y_ref[:, : k * PW], joined)
-        t_hi, t_lo = split_hi_lo(target)
-        i_hi, i_lo = split_hi_lo(inv_ref[k])
-        solved = dot_nt(
-            jnp.concatenate([t_hi, t_hi, t_lo], axis=1), jnp.concatenate([i_hi, i_lo, i_hi], axis=1)
-        )
-        y_ref[:, k * PW : (k + 1) * PW] = solved.astype(jnp.bfloat16)
 
 
 def combine(dense, tiles, write):
@@ -74,10 +47,11 @@
             write(j, cols, acc[j])
 
 
-def exchange_kernel(
-    idx_s, pages, own, base, out,
+def schur_kernel(
+    owner_s, slot_s, c_hbm, inv_hbm, a_hbm, base_hbm, out,
+    c_v, inv_v, a_v, base, own, seats_v, seats_s, pages,
     G, S, RA, T, B1, B2, B3, B4, C3, C4, tiles, RL, L1, L2,
-    sy, ry, sa, sf, ra, rt, sz, rz, sl, rl, rlz,
+    ld, sy, ry, sa, sf, ra, rt, sz, rz, sl, rl, rlz,
 ):
     s = lax.axis_index("sub")
     t = lax.axis_index("tile")
@@ -143,9 +117,9 @@
         elif h == 2:
             src, dst = RA.at[q, zat(3 * sign)], B2.at[d, q, pl.ds(4, 8)]
         elif h == 3:
-            src, dst = C3.at[d, q], B3.at[d, q]
+            src, dst = C3.at[d, lax.rem(q, RING)], B3.at[d, q]
         else:
-            src, dst = C4.at[d, q], B4.at[d, q]
+            src, dst = C4.at[d, lax.rem(q, RING)], B4.at[d, q]
         return rc(src, dst, sz.at[q, d * 5 + h], rz.at[q, d * 5 + h], dev)
 
     def label_group(i):
@@ -163,34 +137,92 @@
             src, dst = RL.at[zat(4), pl.ds(4 * d, 4)], L2.at[d]
         return rc(src, dst, sl.at[7 + 2 * d + i], rlz.at[2 * d + i], at(0, sign * (1 + i), c, 0))
 
+    def loads(k):
+        rows = pl.ds(k * PW, PW)
+        copies = [
+            pltpu.make_async_copy(a_hbm.at[rows], a_v.at[rows], ld.at[k, 0]),
+            pltpu.make_async_copy(inv_hbm.at[k], inv_v.at[k], ld.at[k, 1]),
+        ]
+        if k:
+            blocks = pl.ds(k * (k - 1) // 2, k)
+            copies.append(pltpu.make_async_copy(c_hbm.at[blocks], c_v.at[blocks], ld.at[k, 2]))
+        return copies
+
+    def solve_panel(k, first, last):
+        count = 3 * (last - first) * R
+        cols = slice(k * PW, (k + 1) * PW)
+        target = own[:, first:last, :, cols].reshape(count, PW).astype(jnp.float32)
+        if k:
+            start = k * (k - 1) // 2
+            joined = jnp.concatenate([c_v[start + m] for m in range(k)], axis=1)
+            target = target - dot_nt(own[:, first:last, :, : k * PW].reshape(count, k * PW), joined)
+        t_hi, t_lo = split_hi_lo(target)
+        i_hi, i_lo = split_hi_lo(inv_v[k])
+        solved = dot_nt(
+            jnp.concatenate([t_hi, t_hi, t_lo], axis=1), jnp.concatenate([i_hi, i_lo, i_hi], axis=1)
+        )
+        own[:, first:last, :, cols] = solved.astype(jnp.bfloat16).reshape(3, last - first, R, PW)
+
+    def gather_chunk(q):
+        for i in range(2):
+            y_direct(q, i).wait_recv()
+            y_forward(q, i).start()
+
+    for k in range(8):
+        for copy in loads(k):
+            copy.start()
+    base_load = pltpu.make_async_copy(base_hbm, base, ld.at[8, 0])
+    base_load.start()
+
     barrier = pltpu.get_barrier_semaphore()
     peers = [at(dx, 0, core, 0) for dx, core in direct + two]
     peers += [at(0, dz, c, 0) for dz in (1, -1, 2, -2)] + [at(0, 0, c, dt) for dt in (1, -1)]
     for dev in peers:
         pl.semaphore_signal(barrier, inc=1, device_id=dev, device_id_type=MESH)
+
+    for k in range(8):
+        for copy in loads(k):
+            copy.wait()
+        cols = slice(k * PW, (k + 1) * PW)
+        rows = a_v[cols, :].T
+        own[:, :, :, cols] = rows.reshape(3, NQ, R, PW)
+        solve_panel(k, 0, FIRST)
     pl.semaphore_wait(barrier, len(peers))
-
     for i in range(2):
         y_direct(0, i).start()
+
+    lane = lax.broadcasted_iota(jnp.int32, (8, 128), 1)
+    seat_tile = jnp.full((8, 128), 36, jnp.int32)
+    seat_slot = jnp.full((8, 128), -1, jnp.int32)
+    for a in range(12):
+        d = lax.rem(a // 3 - t + NY, NY)
+        rel = jnp.where(d == 0, 0, jnp.where(d == 3, 1, jnp.where(d == 1, 2, 3)))
+        for b in range(3):
+            o = owner_s[b, 0, a]
+            seat = ((o // 16) * 2 + lax.rem(o, 2)) * 8 + lax.rem(o // 2, 8)
+            here = lane == seat
+            seat_tile = jnp.where(here, (rel * 3 + a % 3) * 3 + b, seat_tile)
+            seat_slot = jnp.where(here, slot_s[b, 0, a], seat_slot)
+    seats_v[0] = seat_tile
+    seats_v[1] = seat_slot
+    to_scalar = pltpu.make_async_copy(seats_v, seats_s, ld.at[8, 1])
+    to_scalar.start()
+    to_scalar.wait()
+    for j in range(64):
+        pages[j // 8, j % 8] = jnp.full((8, 128), seats_s[1, 0, j], jnp.int32)
     for i in range(7):
         label_group(i).start()
+    for k in range(8):
+        solve_panel(k, FIRST, NQ)
+        if k == 5:
+            gather_chunk(0)
+            for q in (1, 2):
+                for i in range(2):
+                    y_direct(q, i).start()
     tiles[36] = jnp.zeros((R, PW), jnp.bfloat16)
     for zz in range(NZ):
         RL[zz, g_own] = pages[g_own, zz]
-    for i in range(1, 8):
-        label_arrival(lax.rem(g_own + i, 8)).wait_recv()
-    for d in range(2):
-        for i in range(2):
-            label_z(d, i).start()
-    for i in range(2):
-        y_direct(0, i).wait_recv()
-        y_forward(0, i).start()
-    for q in (1, 2):
-        for i in range(2):
-            y_direct(q, i).start()
-    for d in range(2):
-        for i in range(2):
-            label_z(d, i).wait_recv()
+    base_load.wait()
 
     def tile_view(ref, *index):
         return lambda cols: ref[(*index, slice(None), cols)]
@@ -226,8 +258,12 @@
                 sign = 1 - 2 * d
                 z_copy(q, d, 3).wait_recv()
 
+                @pl.when(q >= RING)
+                def _(d=d):
+                    z_copy(q - RING, d, 4).wait_send()
+
                 def write(j, cols, value, d=d):
-                    C4[d, q, j, :, cols] = value.astype(jnp.bfloat16)
+                    C4[d, lax.rem(q, RING), j, :, cols] = value.astype(jnp.bfloat16)
 
                 combine(
                     [lambda j, cols, d=d: B3[d, q, j, :, cols]],
@@ -242,8 +278,12 @@
                 z_copy(q, d, 1).wait_recv()
                 z_copy(q, d, 2).wait_recv()
 
+                @pl.when(q >= RING)
+                def _(d=d):
+                    z_copy(q - RING, d, 3).wait_send()
+
                 def write(j, cols, value, d=d):
-                    C3[d, q, j, :, cols] = value.astype(jnp.bfloat16)
+                    C3[d, lax.rem(q, RING), j, :, cols] = value.astype(jnp.bfloat16)
 
                 combine(
                     [],
@@ -282,7 +322,7 @@
                 for p in range(12):
                     tiles[p * 3 + b] = (-gram[p * R : (p + 1) * R]).astype(jnp.bfloat16)
             for j in range(64):
-                S[q, j // 8, j % 8] = tiles[idx_s[j]]
+                S[q, j // 8, j % 8] = tiles[seats_s[0, 0, j]]
             for i in range(2):
                 a_transit(q, i).start()
             for i in range(5):
@@ -290,34 +330,43 @@
             for zz in range(NZ):
                 RA[q, zz, g_own] = S[q, g_own, zz]
 
-        def gather(q):
-            for i in range(2):
-                y_direct(q, i).wait_recv()
-                y_forward(q, i).start()
+        def labels_on():
+            for i in range(1, 8):
+                label_arrival(lax.rem(g_own + i, 8)).wait_recv()
+            for d in range(2):
+                for i in range(2):
+                    label_z(d, i).start()
+
+        def labels_in():
+            for d in range(2):
+                for i in range(2):
+                    label_z(d, i).wait_recv()
 
         def lead(q):
             for i in range(2):
                 y_direct(q, i).start()
 
-        stage(6, finish)
-        stage(5, hop4)
-        stage(4, hop3)
-        stage(3, hop2)
-        stage(2, hop1)
-        stage(1, relay)
+        pl.when(step == 3)(labels_in)
+        stage(5, finish)
+        stage(4, hop4)
+        stage(3, hop3)
+        stage(2, hop2)
         stage(0, form)
 
         @pl.when(step + 1 < NQ)
         def _():
-            gather(step + 1)
+            gather_chunk(step + 1)
 
         @pl.when(step + 3 < NQ)
         def _():
             lead(step + 3)
 
+        stage(1, hop1)
+        stage(0, relay)
+        pl.when(step == 0)(labels_on)
         return carry
 
-    lax.fori_loop(0, NQ + 6, tick, 0)
+    lax.fori_loop(0, NQ + 5, tick, 0)
 
     def drain(q, carry):
         for i in range(2):
@@ -328,11 +377,15 @@
         for i in range(5):
             a_direct(q, i).wait_send()
         for d in range(2):
-            for h in range(5):
+            for h in range(3):
                 z_copy(q, d, h).wait_send()
         return carry
 
     lax.fori_loop(0, NQ, drain, 0)
+    for q in range(NQ - RING, NQ):
+        for d in range(2):
+            for h in (3, 4):
+                z_copy(q, d, h).wait_send()
     for i in range(7):
         label_group(i).wait_send()
     for d in range(2):
@@ -343,27 +396,23 @@
 def shards(coupling, panel_inv, a_ib, owner, slot, base):
     vmem = pl.BlockSpec(memory_space=pltpu.VMEM)
     smem = pl.BlockSpec(memory_space=pltpu.SMEM)
+    hbm = pl.BlockSpec(memory_space=pl.ANY)
     bf16, i32 = jnp.bfloat16, jnp.int32
-    solved, idx, pages = pl.pallas_call(
-        solve_kernel,
-        out_shape=(
-            jax.ShapeDtypeStruct((768, 2048), bf16),
-            jax.ShapeDtypeStruct((64,), i32),
-            jax.ShapeDtypeStruct((8, 8, 8, 128), i32),
-        ),
-        in_specs=[smem, smem, vmem, vmem, vmem],
-        out_specs=(vmem, smem, vmem),
-        scratch_shapes=[pltpu.SMEM((64,), i32)],
-        compiler_params=pltpu.CompilerParams(vmem_limit_bytes=VMEM_LIMIT),
-        name="solve",
-    )(owner[0], slot[0], coupling[0], panel_inv[0], a_ib[0])
     dma = pltpu.SemaphoreType.DMA
     result = pl.pallas_call(
-        exchange_kernel,
+        schur_kernel,
         out_shape=jax.ShapeDtypeStruct((16, PW, PW), bf16),
-        in_specs=[smem, vmem, vmem, vmem],
+        in_specs=[smem, smem, hbm, hbm, hbm, hbm],
         out_specs=vmem,
         scratch_shapes=[
+            pltpu.VMEM((28, PW, PW), bf16),
+            pltpu.VMEM((8, PW, PW), jnp.float32),
+            pltpu.VMEM((2048, 768), bf16),
+            pltpu.VMEM((16, PW, PW), bf16),
+            pltpu.VMEM((3, NQ, R, 2048), bf16),
+            pltpu.VMEM((2, 8, 128), i32),
+            pltpu.SMEM((2, 8, 128), i32),
+            pltpu.VMEM((8, 8, 8, 128), i32),
             pltpu.VMEM((NQ, 3, 3, R, 2048), bf16),
             pltpu.VMEM((NQ, 8, 8, R, PW), bf16),
             pltpu.VMEM((NQ, 8, 8, R, PW), bf16),
@@ -372,12 +421,13 @@
             pltpu.VMEM((2, NQ, 12, R, PW), bf16),
             pltpu.VMEM((2, NQ, 16, R, PW), bf16),
             pltpu.VMEM((2, NQ, 16, R, PW), bf16),
-            pltpu.VMEM((2, NQ, 16, R, PW), bf16),
-            pltpu.VMEM((2, NQ, 16, R, PW), bf16),
+            pltpu.VMEM((2, RING, 16, R, PW), bf16),
+            pltpu.VMEM((2, RING, 16, R, PW), bf16),
             pltpu.VMEM((37, R, PW), bf16),
             pltpu.VMEM((8, 8, 8, 128), i32),
             pltpu.VMEM((2, 8, 8, 128), i32),
             pltpu.VMEM((2, 4, 8, 128), i32),
+            dma((9, 3)),
             dma((NQ, 4)), dma((NQ, 4)),
             dma((NQ, 7)), dma((NQ, 2)), dma((NQ, 8)), dma((NQ, 2)),
             dma((NQ, 10)), dma((NQ, 10)),
@@ -386,8 +436,15 @@
         compiler_params=pltpu.CompilerParams(
             collective_id=0, has_side_effects=True, vmem_limit_bytes=VMEM_LIMIT
         ),
-        name="exchange",
-    )(idx, pages, solved.reshape(3, NQ, R, 2048), base[0])
+        name="schur",
+    )(
+        owner.transpose(2, 0, 1),
+        slot.transpose(2, 0, 1),
+        coupling[0],
+        panel_inv[0],
+        a_ib[0],
+        base[0],
+    )
     return result[None]
 
 

time: 212 us -> 197 us (0.929)
  Pallas kernels: 206 us -> 193 us
  local copies, waits for them, and re-layouts: 5.81 us -> 3.1 us
    pallas_call x2 -> x1, Pallas kernels: 206 us -> 193 us  [shards(): pl.pallas_call(schur_kernel, out_shape=jax.ShapeDtypeStruct((16, PW, PW),...]
    squeeze x2 -> x0, local copies, waits for them, and re-layouts: 2.71 us -> none  [the longest x1 1.36 us: shards(): slot[0]]
where the time goes in v2:
time: 197 us; the launch traced here: 196 us
  Pallas kernels  193 us (98%)
  local copies, waits for them, and re-layouts  3.1 us (2%)
    pallas_call x1, Pallas kernels, shards(): pl.pallas_call(schur_kernel, out_shape=jax.ShapeDtypeStruct((16, PW, PW),...  193 us

profile of v2, /device:TPU:32, one launch (start us, length us, event | category | flops | bytes accessed | tf_op | source)
XLA Modules:
  0.0 196.5 jit_solution(10929423432165184610)
XLA Ops:
  0.0 193.4 %schur.1 = bf16[16,256,256]{2,1,0:T(8,128)(2,1)} custom-call(s32[3,1,12]{2,1,0:T(1,128)} %bitcast.12, s32[3,1,12]{2,1,0:T(1,128)} %bitcast.13, bf16[28,256,256]{2,1,0:T(8,128)(2,1)} %bitcast.8, f32[8,256,256]{2,1,0:T(8,128)} %bitcast.10, bf16[2048,768]{1,0:T(8,128)(2,1)} %bitcast.9, bf16[16,256,256]{2,1,0:T(8,128)(2,1)} %bitcast.11), custom_call_target="tpu_custom_call" | custom-call | tf_op jit(solution)/shard_map/schur/pallas_call | solution.py:402
  193.4 3.1 %copy.8 = bf16[1,16,256,256]{3,2,1,0:T(8,128)(2,1)} copy(bf16[1,16,256,256]{3,2,1,0:T(8,128)(2,1)} %bitcast.7) | data formatting | bytes 4194304

commit v3 on v2

--- a/solution.py
+++ b/solution.py
@@ -51,7 +51,7 @@
     owner_s, slot_s, c_hbm, inv_hbm, a_hbm, base_hbm, out,
     c_v, inv_v, a_v, base, own, seats_v, seats_s, pages,
     G, S, RA, T, B1, B2, B3, B4, C3, C4, tiles, RL, L1, L2,
-    ld, sy, ry, sa, sf, ra, rt, sz, rz, sl, rl, rlz,
+    ld, ss, ry, ra, rt, sz, rz, sl, rl, rlz,
 ):
     s = lax.axis_index("sub")
     t = lax.axis_index("tile")
@@ -66,6 +66,9 @@
     def group(dx, core):
         return lax.rem(x + dx + NX, NX) * 2 + core
 
+    def ring(q):
+        return lax.rem(q, RING)
+
     def zat(dz):
         return lax.rem(z + dz + NZ, NZ)
 
@@ -78,38 +81,39 @@
     two = [(2, 0), (2, 1)]
 
     def y_direct(q, i):
-        return rc(own.at[:, q], G.at[q, i], sy.at[q, i], ry.at[q, i], at(0, 0, c, (1, -1)[i]))
+        return rc(own.at[:, q], G.at[q, i], ss.at[0], ry.at[ring(q), i], at(0, 0, c, (1, -1)[i]))
 
     def y_forward(q, i):
         lanes = pl.ds(i * 1024, 1024)
         return rc(
             G.at[q, i, :, :, lanes], G.at[q, 2, :, :, lanes],
-            sy.at[q, 2 + i], ry.at[q, 2 + i], at(0, 0, c, (1, -1)[i]),
+            ss.at[0], ry.at[ring(q), 2 + i], at(0, 0, c, (1, -1)[i]),
         )
 
     def a_direct(q, i):
         dx, core = direct[i]
         return rc(
-            S.at[q, group(dx, core)], RA.at[q, :, g_own], sa.at[q, i], ra.at[q, g_own], at(dx, 0, core, 0)
+            S.at[q, group(dx, core)], RA.at[q, :, g_own], ss.at[1], ra.at[ring(q), g_own], at(dx, 0, core, 0)
         )
 
     def a_transit(q, i):
         return rc(
-            S.at[q, group(2, i)], T.at[q, i], sa.at[q, 5 + i], rt.at[q, i], at((1, -1)[i], 0, c, 0)
+            S.at[q, group(2, i)], T.at[q, i], ss.at[1], rt.at[ring(q), i], at((1, -1)[i], 0, c, 0)
         )
 
     def a_forward(q, i):
         src_g = group((-1, 1)[i], c)
         return rc(
-            T.at[q, i], RA.at[q, :, src_g], sf.at[q, i], ra.at[q, src_g], at((1, -1)[i], 0, i, 0)
+            T.at[q, i], RA.at[q, :, src_g], ss.at[1], ra.at[ring(q), src_g], at((1, -1)[i], 0, i, 0)
         )
 
     def a_arrival(q, g):
-        return rc(S.at[q, g], RA.at[q, :, g], sa.at[q, 0], ra.at[q, g], at(0, 0, 1 - c, 0))
+        return rc(S.at[q, g], RA.at[q, :, g], ss.at[1], ra.at[ring(q), g], at(0, 0, 1 - c, 0))
 
     def z_copy(q, d, h):
         sign = 1 - 2 * d
         dev = at(0, sign, c, 0)
+        send = ss.at[2] if h < 3 else sz.at[ring(q), d * 2 + h - 3]
         if h == 0:
             src, dst = RA.at[q, zat(4), pl.ds(4 * d, 4)], B1.at[d, q]
         elif h == 1:
@@ -117,10 +121,10 @@
         elif h == 2:
             src, dst = RA.at[q, zat(3 * sign)], B2.at[d, q, pl.ds(4, 8)]
         elif h == 3:
-            src, dst = C3.at[d, lax.rem(q, RING)], B3.at[d, q]
+            src, dst = C3.at[d, ring(q)], B3.at[d, q]
         else:
-            src, dst = C4.at[d, lax.rem(q, RING)], B4.at[d, q]
-        return rc(src, dst, sz.at[q, d * 5 + h], rz.at[q, d * 5 + h], dev)
+            src, dst = C4.at[d, ring(q)], B4.at[d, q]
+        return rc(src, dst, send, rz.at[ring(q), d * 5 + h], dev)
 
     def label_group(i):
         dx, core = (direct + two)[i]
@@ -263,7 +267,7 @@
                     z_copy(q - RING, d, 4).wait_send()
 
                 def write(j, cols, value, d=d):
-                    C4[d, lax.rem(q, RING), j, :, cols] = value.astype(jnp.bfloat16)
+                    C4[d, ring(q), j, :, cols] = value.astype(jnp.bfloat16)
 
                 combine(
                     [lambda j, cols, d=d: B3[d, q, j, :, cols]],
@@ -283,7 +287,7 @@
                     z_copy(q - RING, d, 3).wait_send()
 
                 def write(j, cols, value, d=d):
-                    C3[d, lax.rem(q, RING), j, :, cols] = value.astype(jnp.bfloat16)
+                    C3[d, ring(q), j, :, cols] = value.astype(jnp.bfloat16)
 
                 combine(
                     [],
@@ -368,20 +372,8 @@
 
     lax.fori_loop(0, NQ + 5, tick, 0)
 
-    def drain(q, carry):
-        for i in range(2):
-            y_direct(q, i).wait_send()
-            y_forward(q, i).wait_send()
-            a_transit(q, i).wait_send()
-            a_forward(q, i).wait_send()
-        for i in range(5):
-            a_direct(q, i).wait_send()
-        for d in range(2):
-            for h in range(3):
-                z_copy(q, d, h).wait_send()
-        return carry
-
-    lax.fori_loop(0, NQ, drain, 0)
+    for i, whole in enumerate((G, G, B3)):
+        rc(whole, whole, ss.at[i], ss.at[i], at(0, 0, 1 - c, 0)).wait_send()
     for q in range(NQ - RING, NQ):
         for d in range(2):
             for h in (3, 4):
@@ -428,9 +420,9 @@
             pltpu.VMEM((2, 8, 8, 128), i32),
             pltpu.VMEM((2, 4, 8, 128), i32),
             dma((9, 3)),
-            dma((NQ, 4)), dma((NQ, 4)),
-            dma((NQ, 7)), dma((NQ, 2)), dma((NQ, 8)), dma((NQ, 2)),
-            dma((NQ, 10)), dma((NQ, 10)),
+            dma((3,)),
+            dma((RING, 4)), dma((RING, 8)), dma((RING, 2)),
+            dma((RING, 4)), dma((RING, 10)),
             dma((11,)), dma((8,)), dma((4,)),
         ],
         compiler_params=pltpu.CompilerParams(

time: 197 us -> 190 us (0.964)
  Pallas kernels: 193 us -> 187 us
    pallas_call x1, Pallas kernels: 193 us -> 187 us  [shards(): pl.pallas_call(schur_kernel, out_shape=jax.ShapeDtypeStruct((16, PW, PW),...]
where the time goes in v3:
time: 190 us
  Pallas kernels  187 us (98%)
  local copies, waits for them, and re-layouts  3.1 us (2%)
    pallas_call x1, Pallas kernels, shards(): pl.pallas_call(schur_kernel, out_shape=jax.ShapeDtypeStruct((16, PW, PW),...  187 us

profile of v3, /device:TPU:32, one launch (start us, length us, event | category | flops | bytes accessed | tf_op | source)
XLA Modules:
  0.0 190.3 jit_solution(3070919782407832004)
XLA Ops:
  0.0 187.2 %schur.1 = bf16[16,256,256]{2,1,0:T(8,128)(2,1)} custom-call(s32[3,1,12]{2,1,0:T(1,128)} %bitcast.12, s32[3,1,12]{2,1,0:T(1,128)} %bitcast.13, bf16[28,256,256]{2,1,0:T(8,128)(2,1)} %bitcast.8, f32[8,256,256]{2,1,0:T(8,128)} %bitcast.10, bf16[2048,768]{1,0:T(8,128)(2,1)} %bitcast.9, bf16[16,256,256]{2,1,0:T(8,128)(2,1)} %bitcast.11), custom_call_target="tpu_custom_call" | custom-call | tf_op jit(solution)/shard_map/schur/pallas_call | solution.py:394
  187.2 3.1 %copy.8 = bf16[1,16,256,256]{3,2,1,0:T(8,128)(2,1)} copy(bf16[1,16,256,256]{3,2,1,0:T(8,128)(2,1)} %bitcast.7) | data formatting | bytes 4194304

commit v4 on v3

--- a/solution.py
+++ b/solution.py
@@ -14,7 +14,7 @@
 R = PW // NQ
 FIRST = 4
 RING = 4
-VMEM_LIMIT = 67043328
+VMEM_LIMIT = 59 * 2**20
 NT = (((1,), (1,)), ((), ()))
 
 
@@ -80,14 +80,18 @@
     direct = [(1, 0), (1, 1), (-1, 0), (-1, 1), (0, 1 - c)]
     two = [(2, 0), (2, 1)]
 
-    def y_direct(q, i):
-        return rc(own.at[:, q], G.at[q, i], ss.at[0], ry.at[ring(q), i], at(0, 0, c, (1, -1)[i]))
+    def y_direct(q, i, part):
+        lanes = pl.ds(1024 * (i if part == 0 else 1 - i), 1024)
+        return rc(
+            own.at[:, q, :, lanes], G.at[q, i, :, :, lanes],
+            ss.at[0], ry.at[ring(q), 2 * i + part], at(0, 0, c, (1, -1)[i]),
+        )
 
     def y_forward(q, i):
         lanes = pl.ds(i * 1024, 1024)
         return rc(
             G.at[q, i, :, :, lanes], G.at[q, 2, :, :, lanes],
-            ss.at[0], ry.at[ring(q), 2 + i], at(0, 0, c, (1, -1)[i]),
+            ss.at[0], ry.at[ring(q), 4 + i], at(0, 0, c, (1, -1)[i]),
         )
 
     def a_direct(q, i):
@@ -167,16 +171,20 @@
         )
         own[:, first:last, :, cols] = solved.astype(jnp.bfloat16).reshape(3, last - first, R, PW)
 
+    def lead(q):
+        for part in range(2):
+            for i in range(2):
+                y_direct(q, i, part).start()
+
     def gather_chunk(q):
         for i in range(2):
-            y_direct(q, i).wait_recv()
+            y_direct(q, i, 0).wait_recv()
             y_forward(q, i).start()
 
     for k in range(8):
         for copy in loads(k):
             copy.start()
     base_load = pltpu.make_async_copy(base_hbm, base, ld.at[8, 0])
-    base_load.start()
 
     barrier = pltpu.get_barrier_semaphore()
     peers = [at(dx, 0, core, 0) for dx, core in direct + two]
@@ -191,9 +199,9 @@
         rows = a_v[cols, :].T
         own[:, :, :, cols] = rows.reshape(3, NQ, R, PW)
         solve_panel(k, 0, FIRST)
+    base_load.start()
     pl.semaphore_wait(barrier, len(peers))
-    for i in range(2):
-        y_direct(0, i).start()
+    lead(0)
 
     lane = lax.broadcasted_iota(jnp.int32, (8, 128), 1)
     seat_tile = jnp.full((8, 128), 36, jnp.int32)
@@ -220,9 +228,7 @@
         solve_panel(k, FIRST, NQ)
         if k == 5:
             gather_chunk(0)
-            for q in (1, 2):
-                for i in range(2):
-                    y_direct(q, i).start()
+            lead(1)
     tiles[36] = jnp.zeros((R, PW), jnp.bfloat16)
     for zz in range(NZ):
         RL[zz, g_own] = pages[g_own, zz]
@@ -317,6 +323,7 @@
 
         def form(q):
             for i in range(2):
+                y_direct(q, i, 1).wait_recv()
                 y_forward(q, i).wait_recv()
             left = jnp.concatenate(
                 [own[:, q].reshape(3 * R, 2048), G[q].reshape(9 * R, 2048)], axis=0
@@ -346,31 +353,27 @@
                 for i in range(2):
                     label_z(d, i).wait_recv()
 
-        def lead(q):
-            for i in range(2):
-                y_direct(q, i).start()
-
-        pl.when(step == 3)(labels_in)
-        stage(5, finish)
-        stage(4, hop4)
-        stage(3, hop3)
+        pl.when(step == 2)(labels_in)
         stage(2, hop2)
-        stage(0, form)
+        pl.when(step == 1)(labels_on)
+        stage(1, relay)
+        stage(6, finish)
 
         @pl.when(step + 1 < NQ)
         def _():
             gather_chunk(step + 1)
 
-        @pl.when(step + 3 < NQ)
+        @pl.when(step + 2 < NQ)
         def _():
-            lead(step + 3)
-
+            lead(step + 2)
+
+        stage(0, form)
+        stage(4, hop4)
         stage(1, hop1)
-        stage(0, relay)
-        pl.when(step == 0)(labels_on)
+        stage(2, hop3)
         return carry
 
-    lax.fori_loop(0, NQ + 5, tick, 0)
+    lax.fori_loop(0, NQ + 6, tick, 0)
 
     for i, whole in enumerate((G, G, B3)):
         rc(whole, whole, ss.at[i], ss.at[i], at(0, 0, 1 - c, 0)).wait_send()
@@ -393,7 +396,7 @@
     dma = pltpu.SemaphoreType.DMA
     result = pl.pallas_call(
         schur_kernel,
-        out_shape=jax.ShapeDtypeStruct((16, PW, PW), bf16),
+        out_shape=pltpu.VMEM((16, PW, PW), bf16),
         in_specs=[smem, smem, hbm, hbm, hbm, hbm],
         out_specs=vmem,
         scratch_shapes=[
@@ -421,7 +424,7 @@
             pltpu.VMEM((2, 4, 8, 128), i32),
             dma((9, 3)),
             dma((3,)),
-            dma((RING, 4)), dma((RING, 8)), dma((RING, 2)),
+            dma((RING, 6)), dma((RING, 8)), dma((RING, 2)),
             dma((RING, 4)), dma((RING, 10)),
             dma((11,)), dma((8,)), dma((4,)),
         ],

time: 190 us -> 182 us (0.958)
  Pallas kernels: 187 us -> 180 us
    pallas_call x1, Pallas kernels: 187 us -> 180 us  [shards(): pl.pallas_call(schur_kernel, out_shape=pltpu.VMEM((16, PW, PW), bf16), in...]
where the time goes in v4:
time: 182 us
  Pallas kernels  180 us (99%)
    pallas_call x1, Pallas kernels, shards(): pl.pallas_call(schur_kernel, out_shape=pltpu.VMEM((16, PW, PW), bf16), in...  180 us

profile of v4, /device:TPU:32, one launch (start us, length us, event | category | flops | bytes accessed | tf_op | source)
XLA Modules:
  0.0 181.8 jit_solution(2427650833562593317)
XLA Ops:
  0.0 180.5 %schur.1 = bf16[16,256,256]{2,1,0:T(8,128)(2,1)S(1)} custom-call(s32[3,1,12]{2,1,0:T(1,128)} %bitcast.12, s32[3,1,12]{2,1,0:T(1,128)} %bitcast.13, bf16[28,256,256]{2,1,0:T(8,128)(2,1)} %bitcast.8, f32[8,256,256]{2,1,0:T(8,128)} %bitcast.10, bf16[2048,768]{1,0:T(8,128)(2,1)} %bitcast.9, bf16[16,256,256]{2,1,0:T(8,128)(2,1)} %bitcast.11), custom_call_target="tpu_custom_call" | custom-call | tf_op jit(solution)/shard_map/schur/pallas_call | solution.py:397
  180.5 1.3 copy.8

commit v5 on v4

--- a/solution.py
+++ b/solution.py
@@ -354,10 +354,8 @@
                     label_z(d, i).wait_recv()
 
         pl.when(step == 2)(labels_in)
-        stage(2, hop2)
+        stage(1, relay)
         pl.when(step == 1)(labels_on)
-        stage(1, relay)
-        stage(6, finish)
 
         @pl.when(step + 1 < NQ)
         def _():
@@ -367,9 +365,11 @@
         def _():
             lead(step + 2)
 
+        stage(2, hop2)
         stage(0, form)
+        stage(1, hop1)
+        stage(6, finish)
         stage(4, hop4)
-        stage(1, hop1)
         stage(2, hop3)
         return carry
 

time: 182 us -> 181 us (level)
  Pallas kernels: 180 us -> 178 us
    pallas_call x1, Pallas kernels: 180 us -> 178 us  [shards(): pl.pallas_call(schur_kernel, out_shape=pltpu.VMEM((16, PW, PW), bf16), in...]
where the time goes in v5:
time: 181 us; the launch traced here: 179 us
  Pallas kernels  178 us (98%)
    pallas_call x1, Pallas kernels, shards(): pl.pallas_call(schur_kernel, out_shape=pltpu.VMEM((16, PW, PW), bf16), in...  178 us

profile of v5, /device:TPU:32, one launch (start us, length us, event | category | flops | bytes accessed | tf_op | source)
XLA Modules:
  0.0 179.2 jit_solution(4218151849946371589)
XLA Ops:
  0.0 177.9 %schur.1 = bf16[16,256,256]{2,1,0:T(8,128)(2,1)S(1)} custom-call(s32[3,1,12]{2,1,0:T(1,128)} %bitcast.12, s32[3,1,12]{2,1,0:T(1,128)} %bitcast.13, bf16[28,256,256]{2,1,0:T(8,128)(2,1)} %bitcast.8, f32[8,256,256]{2,1,0:T(8,128)} %bitcast.10, bf16[2048,768]{1,0:T(8,128)(2,1)} %bitcast.9, bf16[16,256,256]{2,1,0:T(8,128)(2,1)} %bitcast.11), custom_call_target="tpu_custom_call" | custom-call | tf_op jit(solution)/shard_map/schur/pallas_call | solution.py:397
  177.9 1.3 copy.8

commit v6 on v5

--- a/solution.py
+++ b/solution.py
@@ -332,14 +332,19 @@
                 gram = dot_nt(left, own[b].reshape(PW, 2048))
                 for p in range(12):
                     tiles[p * 3 + b] = (-gram[p * R : (p + 1) * R]).astype(jnp.bfloat16)
-            for j in range(64):
-                S[q, j // 8, j % 8] = tiles[seats_s[0, 0, j]]
+            def pack(dst, g):
+                for zz in range(NZ):
+                    dst(zz)[...] = tiles[seats_s[0, 0, g * NZ + zz]]
+
             for i in range(2):
+                far = group(2, i)
+                pack(lambda zz, far=far: S.at[q, far, zz], far)
                 a_transit(q, i).start()
             for i in range(5):
+                near = group(*direct[i])
+                pack(lambda zz, near=near: S.at[q, near, zz], near)
                 a_direct(q, i).start()
-            for zz in range(NZ):
-                RA[q, zz, g_own] = S[q, g_own, zz]
+            pack(lambda zz: RA.at[q, zz, g_own], g_own)
 
         def labels_on():
             for i in range(1, 8):

time: 181 us -> 181 us (level)
  no operation moved by 1% of the time
where the time goes in v6:
time: 181 us; the launch traced here: 179 us
  Pallas kernels  178 us (98%)
    pallas_call x1, Pallas kernels, shards(): pl.pallas_call(schur_kernel, out_shape=pltpu.VMEM((16, PW, PW), bf16), in...  178 us

profile of v6, /device:TPU:32, one launch (start us, length us, event | category | flops | bytes accessed | tf_op | source)
XLA Modules:
  0.0 179.2 jit_solution(11698053423671612683)
XLA Ops:
  0.0 177.9 %schur.1 = bf16[16,256,256]{2,1,0:T(8,128)(2,1)S(1)} custom-call(s32[3,1,12]{2,1,0:T(1,128)} %bitcast.12, s32[3,1,12]{2,1,0:T(1,128)} %bitcast.13, bf16[28,256,256]{2,1,0:T(8,128)(2,1)} %bitcast.8, f32[8,256,256]{2,1,0:T(8,128)} %bitcast.10, bf16[2048,768]{1,0:T(8,128)(2,1)} %bitcast.9, bf16[16,256,256]{2,1,0:T(8,128)(2,1)} %bitcast.11), custom_call_target="tpu_custom_call" | custom-call | tf_op jit(solution)/shard_map/schur/pallas_call | solution.py:402
  177.9 1.3 copy.8
